TPU v7x, 32 devices: a whole 2x2x4 slice. The times are simulated.
32 devices in a mesh: rows: 4 (over x, core), cols: 8 (over z, y).
Axes of the slice: x: 2, y: 2, z: 4, core: 2. Of those that a mesh axis runs over, the one named last changes fastest.
Arguments:
- elevation: float32 [512, 8192], P('rows', 'cols'), may hold values from -6 to 6
- data_mask: int32 [512, 8192], P('rows', 'cols'), may hold values 0 or 1
- tie_order: int32 [8], replicated, may hold values from 0 to 7, each once
Outputs:
- inflow: float32 [512, 8192], P('rows', 'cols')
Inputs may be any that keep to these rules, and one draw needn't show every extreme that they name: tie_order holds each of 0 to 7 once.
All inputs are finite; a program needn't handle non-finite values. No bound on the sum of `data_mask` on one device may be relied on, other than what follows from the above.
Results may differ from a plain program's by a relative error of at most 0.0003.
Values sent between devices are 32-bit elements; how exact they have to be, the bound alone decides.
A program may use at most 64 MiB of HBM per device.

v0:
```python
import jax
import jax.numpy as jnp
from jax import lax
from jax.sharding import PartitionSpec as P

ITERS = 8


OFFSETS = ((0, 1), (1, 1), (1, 0), (1, -1), (0, -1), (-1, -1), (-1, 0), (-1, 1))
RECIPROCAL = (
    1.0,
    0.7071067811865476,
    1.0,
    0.7071067811865476,
    1.0,
    0.7071067811865476,
    1.0,
    0.7071067811865476,
)
RETENTION = 0.1


def with_halo(cells, sides, width):
    for axis, dim in sides:
        count = lax.axis_size(axis)
        ends = count - 1
        head = lax.slice_in_dim(cells, 0, width, axis=dim)
        tail = lax.slice_in_dim(cells, cells.shape[dim] - width, cells.shape[dim], axis=dim)
        cells = jnp.concatenate(
            [
                lax.ppermute(tail, axis, [(i, (i + 1) % count) for i in range(ends)]),
                cells,
                lax.ppermute(head, axis, [((i + 1) % count, i) for i in range(ends)]),
            ],
            axis=dim,
        )
    return cells


def priorities(tie_order):
    places = jnp.arange(8, dtype=jnp.float32)
    values = 1.0 + 0.5 * (7.0 - places) / 7.0
    matches = (tie_order[:, None] == jnp.arange(8, dtype=jnp.int32)[None, :]).astype(jnp.float32)
    return jnp.sum(matches * values[:, None], axis=0)


def outflow_weight_matrix(height_pad, valid_pad, ranking_order):
    height = height_pad.shape[0] - 2
    breadth = height_pad.shape[1] - 2
    centre = height_pad[1:-1, 1:-1]
    slopes = []
    for number, (step_row, step_col) in enumerate(OFFSETS):
        beside = height_pad[
            1 + step_row : 1 + step_row + height, 1 + step_col : 1 + step_col + breadth
        ]
        beside_ok = valid_pad[
            1 + step_row : 1 + step_row + height, 1 + step_col : 1 + step_col + breadth
        ]
        slopes.append(
            beside_ok
            * ranking_order[number]
            * jnp.maximum(centre - beside, 0.0)
            * RECIPROCAL[number]
        )
    slopes = jnp.stack(slopes)
    totals = jnp.sum(slopes, axis=0) + RETENTION
    return slopes / totals


def gather_inflow(weights, field_pad):
    height = field_pad.shape[0] - 2
    breadth = field_pad.shape[1] - 2
    summed_in = jnp.zeros((height, breadth), jnp.float32)
    for number, (step_row, step_col) in enumerate(OFFSETS):
        term = weights[number] * field_pad
        summed_in = (
            summed_in
            + term[1 - step_row : 1 - step_row + height, 1 - step_col : 1 - step_col + breadth]
        )
    return summed_in


def edge_valid(position, length, devices, margin):
    places = position * length + jnp.arange(length + 2 * margin, dtype=jnp.int32) - margin
    return ((places >= 0) & (places < length * devices)).astype(jnp.float32)


def trimmed(field, cut):
    return field[..., cut : field.shape[-2] - cut, cut : field.shape[-1] - cut]


def on_device(elevation, data_mask, tie_order):
    ranking_order = priorities(tie_order)
    row_index = lax.axis_index("rows")
    col_index = lax.axis_index("cols")
    row_devices = lax.axis_size("rows")
    col_devices = lax.axis_size("cols")
    tile_rows, tile_cols = elevation.shape
    coarse_rows, coarse_cols = (tile_rows // 8, tile_cols // 8)
    valid_flag = data_mask.astype(jnp.float32)
    summed = (valid_flag * elevation).reshape(coarse_rows, 8, coarse_cols, 8).sum(axis=(1, 3))
    counts = valid_flag.reshape(coarse_rows, 8, coarse_cols, 8).sum(axis=(1, 3))
    overview = summed / (counts + 1.0)
    runoff = counts / 64.0
    elevation_window = with_halo(elevation, (("rows", 0), ("cols", 1)), 2)
    depth = ITERS + 2
    over_win, runoff_win = (
        with_halo(overview, (("rows", 0), ("cols", 1)), depth),
        with_halo(runoff, (("rows", 0), ("cols", 1)), depth),
    )
    window_valid = (
        edge_valid(row_index, coarse_rows, row_devices, depth)[:, None]
        * edge_valid(col_index, coarse_cols, col_devices, depth)[None, :]
    )
    coarse_w = outflow_weight_matrix(over_win, window_valid, ranking_order)
    flow_now = trimmed(runoff_win, 1)
    for sweep in range(ITERS):
        flow_now = trimmed(runoff_win, sweep + 2) + gather_inflow(
            trimmed(coarse_w, sweep), flow_now
        )
        flow_now = flow_now * trimmed(window_valid, sweep + 2)
    upsampled = jnp.repeat(jnp.repeat(flow_now, 8, axis=0), 8, axis=1)
    up_window = upsampled[7 : 7 + tile_rows + 2, 7 : 7 + tile_cols + 2]
    detailed_valid = (
        edge_valid(row_index, tile_rows, row_devices, 2)[:, None]
        * edge_valid(col_index, tile_cols, col_devices, 2)[None, :]
    )
    detailed_weight = outflow_weight_matrix(elevation_window, detailed_valid, ranking_order)
    return valid_flag + gather_inflow(detailed_weight, up_window)


def solution(mesh):
    in_specs = (P("rows", "cols"), P("rows", "cols"), P())
    out_specs = P("rows", "cols")
    return jax.shard_map(
        on_device, mesh=mesh, in_specs=in_specs, out_specs=out_specs, check_vma=False
    )
```

profile of v0, /device:TPU:6, one launch (start us, length us, event | category | flops | bytes accessed | tf_op | source)
XLA Modules:
  0.0 103.3 jit_solution(837099264817420682)
XLA Ops:
  0.0 0.8 fusion.133
  0.8 1.0 %copy.22 = f32[2,1024]{0,1:T(8,128)} copy(f32[2,1024]{1,0:T(2,128)S(1)} %get-tuple-element.35) | data formatting | bytes 16384 | tf_op jit(solution)/shard_map/slice | solution.py:28
  1.9 1.9 %collective-permute-start = (f32[2,1024]{0,1:T(8,128)}, f32[2,1024]{0,1:T(8,128)S(1)}, u32[]{:S(2)}, u32[]{:S(2)}) collective-permute-start(f32[2,1024]{0,1:T(8,128)} %copy.22), channel_id=1, source_target_pairs={{0,8},{8,16},{16,24},{1,9},{9,17},{17,25},{2,10},{10,18},{18,26},{... | collective-permute-start | bytes 24584 | tf_op jit(solution)/shard_map/ppermute | solution.py:31
  3.8 1.0 %copy.23 = f32[2,1024]{0,1:T(8,128)} copy(f32[2,1024]{1,0:T(2,128)S(1)} %get-tuple-element.36) | data formatting | bytes 16384 | tf_op jit(solution)/shard_map/slice | solution.py:27
  4.8 3.6 %collective-permute-start.1 = (f32[2,1024]{0,1:T(8,128)}, f32[2,1024]{0,1:T(8,128)S(1)}, u32[]{:S(2)}, u32[]{:S(2)}) collective-permute-start(f32[2,1024]{0,1:T(8,128)} %copy.23), channel_id=1, source_target_pairs={{8,0},{16,8},{24,16},{9,1},{17,9},{25,17},{10,2},{18,10},{26,18},{... | collective-permute-start | bytes 24584 | tf_op jit(solution)/shard_map/ppermute | solution.py:33
  8.5 0.2 copy.24
  8.7 0.2 copy.21
  8.9 0.9 convert_element_type.32
  9.9 0.2 copy.27
  10.1 6.2 %reshape.122 = f32[16,8,128,8]{3,2,1,0:T(8,128)} reshape(f32[128,1024]{1,0:T(8,128)S(1)} %copy.27) | data formatting | bytes 1048576 | tf_op jit(solution)/shard_map/reshape | solution.py:101
  16.3 0.2 copy.25
  16.5 6.1 %reshape.121 = f32[16,8,128,8]{3,2,1,0:T(8,128)} reshape(f32[128,1024]{1,0:T(8,128)S(1)} %copy.25) | data formatting | bytes 1048576 | tf_op jit(solution)/shard_map/reshape | solution.py:102
  22.7 4.0 %reduce_sum.100 = f32[16,128]{1,0:T(8,128)S(1)} reduce(f32[16,8,128,8]{3,2,1,0:T(8,128)} %reshape.122, f32[]{:T(128)} %constant.29.clone.1), dimensions={1,3}, to_apply=%region_2.0 | reduce | flops 129024 | bytes 532484 | tf_op jit(solution)/shard_map/reduce_sum | solution.py:101
  26.7 4.0 %reduce_sum.99 = f32[16,128]{1,0:T(8,128)S(1)} reduce(f32[16,8,128,8]{3,2,1,0:T(8,128)} %reshape.121, f32[]{:T(128)} %constant.29.clone.1), dimensions={1,3}, to_apply=%region_1.0 | reduce | flops 129024 | bytes 532484 | tf_op jit(solution)/shard_map/reduce_sum | solution.py:102
  30.7 1.9 %collective-permute-start.8 = (f32[10,128]{1,0:T(8,128)S(1)}, f32[10,128]{1,0:T(8,128)S(1)}, u32[]{:S(2)}, u32[]{:S(2)}) collective-permute-start(f32[10,128]{1,0:T(8,128)S(1)} %get-tuple-element.105), channel_id=1, source_target_pairs={{0,8},{8,16},{16,24},{1,9},{9,17},{17,25},{2,10},{10,18},{18,26},{... | collective-permute-start | bytes 15368 | tf_op jit(solution)/shard_map/ppermute | solution.py:31
  32.6 3.6 %collective-permute-start.9 = (f32[10,128]{1,0:T(8,128)S(1)}, f32[10,128]{1,0:T(8,128)S(1)}, u32[]{:S(2)}, u32[]{:S(2)}) collective-permute-start(f32[10,128]{1,0:T(8,128)S(1)} %get-tuple-element.106), channel_id=1, source_target_pairs={{8,0},{16,8},{24,16},{9,1},{17,9},{25,17},{10,2},{18,10},{26,18},{... | collective-permute-start | bytes 15368 | tf_op jit(solution)/shard_map/ppermute | solution.py:33
  36.3 1.9 %collective-permute-start.4 = (f32[10,128]{1,0:T(8,128)S(1)}, f32[10,128]{1,0:T(8,128)S(1)}, u32[]{:S(2)}, u32[]{:S(2)}) collective-permute-start(f32[10,128]{1,0:T(8,128)S(1)} %get-tuple-element.109), channel_id=1, source_target_pairs={{0,8},{8,16},{16,24},{1,9},{9,17},{17,25},{2,10},{10,18},{18,26},{... | collective-permute-start | bytes 15368 | tf_op jit(solution)/shard_map/ppermute | solution.py:31
  38.4 0.2 broadcast_multiply_fusion
  38.7 0.7 fusion.138
  39.4 3.6 %collective-permute-start.5 = (f32[10,128]{1,0:T(8,128)S(1)}, f32[10,128]{1,0:T(8,128)S(1)}, u32[]{:S(2)}, u32[]{:S(2)}) collective-permute-start(f32[10,128]{1,0:T(8,128)S(1)} %get-tuple-element.110), channel_id=1, source_target_pairs={{8,0},{16,8},{24,16},{9,1},{17,9},{25,17},{10,2},{18,10},{26,18},{... | collective-permute-start | bytes 15368 | tf_op jit(solution)/shard_map/ppermute | solution.py:33
  43.1 3.4 %collective-permute-start.10 = (f32[36,10]{1,0:T(8,128)S(1)}, f32[36,10]{1,0:T(8,128)S(1)}, u32[]{:S(2)}, u32[]{:S(2)}) collective-permute-start(f32[36,10]{1,0:T(8,128)S(1)} %get-tuple-element.101), channel_id=1, source_target_pairs={{0,1},{1,2},{2,3},{3,4},{4,5},{5,6},{6,7},{8,9},{9,10},{10,11},{11... | collective-permute-start | bytes 4328 | tf_op jit(solution)/shard_map/ppermute | solution.py:31
  46.6 2.4 %collective-permute-start.11 = (f32[36,10]{1,0:T(8,128)S(1)}, f32[36,10]{1,0:T(8,128)S(1)}, u32[]{:S(2)}, u32[]{:S(2)}) collective-permute-start(f32[36,10]{1,0:T(8,128)S(1)} %get-tuple-element.102), channel_id=1, source_target_pairs={{1,0},{2,1},{3,2},{4,3},{5,4},{6,5},{7,6},{9,8},{10,9},{11,10},{12... | collective-permute-start | bytes 4328 | tf_op jit(solution)/shard_map/ppermute | solution.py:33
  49.1 4.3 %collective-permute-start.6 = (f32[36,10]{1,0:T(8,128)S(1)}, f32[36,10]{1,0:T(8,128)S(1)}, u32[]{:S(2)}, u32[]{:S(2)}) collective-permute-start(f32[36,10]{1,0:T(8,128)S(1)} %get-tuple-element.103), channel_id=1, source_target_pairs={{0,1},{1,2},{2,3},{3,4},{4,5},{5,6},{6,7},{8,9},{9,10},{10,11},{11... | collective-permute-start | bytes 4328 | tf_op jit(solution)/shard_map/ppermute | solution.py:31
  53.4 1.9 %collective-permute-start.7 = (f32[36,10]{1,0:T(8,128)S(1)}, f32[36,10]{1,0:T(8,128)S(1)}, u32[]{:S(2)}, u32[]{:S(2)}) collective-permute-start(f32[36,10]{1,0:T(8,128)S(1)} %get-tuple-element.104), channel_id=1, source_target_pairs={{1,0},{2,1},{3,2},{4,3},{5,4},{6,5},{7,6},{9,8},{10,9},{11,10},{12... | collective-permute-start | bytes 4328 | tf_op jit(solution)/shard_map/ppermute | solution.py:33
  55.5 5.1 %add_add_fusion.1 = (f32[34,146]{1,0:T(8,128)S(1)}, f32[34,146]{1,0:T(8,128)S(1)}, f32[34,146]{1,0:T(8,128)S(1)}, f32[34,146]{1,0:T(8,128)S(1)}, f32[34,146]{1,0...) fusion(f32[36,148]{1,0:T(8,128)S(1)} %pad_maximum_fusion.3, ...), kind=kLoop, calls=%fused_computation.131 | loop fusion | flops 218416 | bytes 516288 | tf_op jit(solution)/shard_map/add | solution.py:66
  61.9 0.2 slice_multiply_fusion.51
  62.1 0.2 slice_multiply_fusion.42
  62.2 0.2 slice_multiply_fusion.33
  62.4 0.2 slice_multiply_fusion.24
  62.6 0.1 slice_multiply_fusion.87
  62.8 0.1 slice_multiply_fusion.78
  62.9 0.1 slice_multiply_fusion.69
  63.1 0.1 slice_multiply_fusion.60
  63.4 0.5 pad_maximum_fusion.1
  63.9 0.3 copy-done.4
  64.2 4.8 %collective-permute-start.2 = (f32[132,2]{0,1:T(2,128)S(1)}, f32[132,2]{0,1:T(2,128)S(1)}, u32[]{:S(2)}, u32[]{:S(2)}) collective-permute-start(f32[132,2]{0,1:T(2,128)S(1)} %get-tuple-element.33), channel_id=1, source_target_pairs={{0,1},{1,2},{2,3},{3,4},{4,5},{5,6},{6,7},{8,9},{9,10},{10,11},{11... | collective-permute-start | bytes 3176 | tf_op jit(solution)/shard_map/ppermute | solution.py:31
  69.0 2.1 %collective-permute-start.3 = (f32[132,2]{0,1:T(2,128)S(1)}, f32[132,2]{0,1:T(2,128)S(1)}, u32[]{:S(2)}, u32[]{:S(2)}) collective-permute-start(f32[132,2]{0,1:T(2,128)S(1)} %get-tuple-element.34), channel_id=1, source_target_pairs={{1,0},{2,1},{3,2},{4,3},{5,4},{6,5},{7,6},{9,8},{10,9},{11,10},{12... | collective-permute-start | bytes 3176 | tf_op jit(solution)/shard_map/ppermute | solution.py:33
  71.2 0.3 slice.1195
  71.5 3.8 %collective-permute-done.3 = f32[132,2]{0,1:T(2,128)S(1)} collective-permute-done((f32[132,2]{0,1:T(2,128)S(1)}, f32[132,2]{0,1:T(2,128)S(1)}, u32[]{:S(2)}, u32[]{:S(2)}) %collective-permute-start.3) | collective-permute-done | bytes 1088 | tf_op jit(solution)/shard_map/ppermute | solution.py:33
  75.4 2.2 %maximum_maximum_fusion = (f32[132,1026]{0,1:T(8,128)}, f32[132,1026]{0,1:T(8,128)}) fusion(f32[2,1024]{0,1:T(8,128)S(1)} %copy-done.5, f32[128,1024]{0,1:T(8,128)S(1)} %copy.24, f32[2,1024]{0,1:T(8,128)S(1)} %collective-permute-done, f32[132,2]{0,1:T(2,128)S(1)} %collective-permute-done.2, f32[132,2]{0,1:T(2,128)S(1)} %collective-permute-done.3), kind=kLoop, calls=%fused_computation.46 | loop fusion | flops 812592 | bytes 1626240 | tf_op jit(solution)/shard_map/concatenate | solution.py:29
  77.6 3.2 %concatenate.29 = f32[132,1028]{0,1:T(8,128)S(1)} concatenate(f32[132,2]{0,1:T(2,128)S(1)} %collective-permute-done.2, f32[132,1024]{0,1:T(8,128)} %copy-done.3, f32[132,2]{0,1:T(2,128)S(1)} %collective-permute-done.3), dimensions={1} | concatenate | bytes 1085568 | tf_op jit(solution)/shard_map/concatenate | solution.py:29
  80.8 10.9 %add_add_fusion = (f32[130,1026]{0,1:T(8,128)S(1)}, f32[130,1026]{0,1:T(8,128)S(1)}, f32[130,1026]{0,1:T(8,128)S(1)}, f32[130,1026]{0,1:T(8,128)S(1)}, f32[130,1...) fusion(f32[132,1026]{0,1:T(8,128)} %get-tuple-element.32, ...), kind=kLoop, calls=%fused_computation.55 | loop fusion | flops 5868720 | bytes 13871552 | tf_op jit(solution)/shard_map/add | solution.py:66
  92.4 3.3 %copy-done = f32[8,130,1026]{1,2,0:T(8,128)} copy-done((f32[8,130,1026]{1,2,0:T(8,128)}, f32[8,130,1026]{1,2,0:T(8,128)S(1)}, u32[]{:S(2)}) %copy-start) | copy-done | bytes 4268184
  95.6 4.1 %broadcast_divide_fusion = f32[8,130,1026]{1,2,0:T(8,128)S(1)} fusion(f32[8,130,1026]{1,2,0:T(8,128)} %copy-done, f32[130,1026]{0,1:T(8,128)S(1)} %get-tuple-element.5), kind=kLoop, calls=%fused_computation | loop fusion | flops 1067040 | bytes 9069840 | tf_op jit(solution)/shard_map/div | solution.py:67
  99.8 0.6 slice_bitcast_fusion.7
  100.3 0.5 copy-done.2
  100.8 1.5 %fusion.21 = f32[128,1024]{0,1:T(8,128)S(1)} fusion(f32[130,1026]{0,1:T(8,128)S(1)} %slice.1195, f32[130,1026]{0,1:T(8,128)S(1)} %get-tuple-element.24, f32[130,1026]{0,1:T(8,128)S(1)} %get-tuple-element.25, f32[130,1026]{0,1:T(8,128)S(1)} %get-tuple-element.26, f32[130,1026]{0,1:T(8,128)S(1)} %get-tuple-element.27, f32[130,1026]{0,1:T(8,128)S(1)} %get-tuple-element.28, ...), kind=kLoop, calls=%fused_computation.61 | loop fusion | flops 2228224 | bytes 9437184 | tf_op jit(solution)/shard_map/add | solution.py:129
  102.3 1.0 copy.29
  (75 shorter events, 2.5 us)
Async XLA Ops:
  0.0 8.5 %copy-start.7 = (f32[128,1024]{1,0:T(8,128)S(1)}, f32[128,1024]{1,0:T(8,128)}, u32[]{:S(2)}) copy-start(f32[128,1024]{1,0:T(8,128)} %param.3) | copy-start | bytes 1572868
  0.8 7.9 %copy-start.8 = (s32[128,1024]{1,0:T(8,128)S(1)}, s32[128,1024]{1,0:T(8,128)}, u32[]{:S(2)}) copy-start(s32[128,1024]{1,0:T(8,128)} %param.4) | copy-start | bytes 1572868
  1.9 61.5 %collective-permute-start = (f32[2,1024]{0,1:T(8,128)}, f32[2,1024]{0,1:T(8,128)S(1)}, u32[]{:S(2)}, u32[]{:S(2)}) collective-permute-start(f32[2,1024]{0,1:T(8,128)} %copy.22), channel_id=1, source_target_pairs={{0,8},{8,16},{16,24},{1,9},{9,17},{17,25},{2,10},{10,18},{18,26},{... | collective-permute-start | bytes 24584 | tf_op jit(solution)/shard_map/ppermute | solution.py:31
  4.8 58.5 %collective-permute-start.1 = (f32[2,1024]{0,1:T(8,128)}, f32[2,1024]{0,1:T(8,128)S(1)}, u32[]{:S(2)}, u32[]{:S(2)}) collective-permute-start(f32[2,1024]{0,1:T(8,128)} %copy.23), channel_id=1, source_target_pairs={{8,0},{16,8},{24,16},{9,1},{17,9},{25,17},{10,2},{18,10},{26,18},{... | collective-permute-start | bytes 24584 | tf_op jit(solution)/shard_map/ppermute | solution.py:33
  8.9 1.0 copy-start.1
  10.1 6.2 %copy-start.6 = (f32[128,1024]{0,1:T(8,128)S(1)}, f32[128,1024]{0,1:T(8,128)}, u32[]{:S(2)}) copy-start(f32[128,1024]{0,1:T(8,128)} %convert_element_type.32) | copy-start | bytes 1572868
  26.7 11.7 %copy-start.9 = (s32[8]{0:T(128)S(1)}, s32[8]{0:T(128)}, u32[]{:S(2)}) copy-start(s32[8]{0:T(128)} %param.5) | copy-start | bytes 100
  30.7 8.7 %collective-permute-start.8 = (f32[10,128]{1,0:T(8,128)S(1)}, f32[10,128]{1,0:T(8,128)S(1)}, u32[]{:S(2)}, u32[]{:S(2)}) collective-permute-start(f32[10,128]{1,0:T(8,128)S(1)} %get-tuple-element.105), channel_id=1, source_target_pairs={{0,8},{8,16},{16,24},{1,9},{9,17},{17,25},{2,10},{10,18},{18,26},{... | collective-permute-start | bytes 15368 | tf_op jit(solution)/shard_map/ppermute | solution.py:31
  32.6 10.4 %collective-permute-start.9 = (f32[10,128]{1,0:T(8,128)S(1)}, f32[10,128]{1,0:T(8,128)S(1)}, u32[]{:S(2)}, u32[]{:S(2)}) collective-permute-start(f32[10,128]{1,0:T(8,128)S(1)} %get-tuple-element.106), channel_id=1, source_target_pairs={{8,0},{16,8},{24,16},{9,1},{17,9},{25,17},{10,2},{18,10},{26,18},{... | collective-permute-start | bytes 15368 | tf_op jit(solution)/shard_map/ppermute | solution.py:33
  36.3 10.3 %collective-permute-start.4 = (f32[10,128]{1,0:T(8,128)S(1)}, f32[10,128]{1,0:T(8,128)S(1)}, u32[]{:S(2)}, u32[]{:S(2)}) collective-permute-start(f32[10,128]{1,0:T(8,128)S(1)} %get-tuple-element.109), channel_id=1, source_target_pairs={{0,8},{8,16},{16,24},{1,9},{9,17},{17,25},{2,10},{10,18},{18,26},{... | collective-permute-start | bytes 15368 | tf_op jit(solution)/shard_map/ppermute | solution.py:31
  39.4 9.6 %collective-permute-start.5 = (f32[10,128]{1,0:T(8,128)S(1)}, f32[10,128]{1,0:T(8,128)S(1)}, u32[]{:S(2)}, u32[]{:S(2)}) collective-permute-start(f32[10,128]{1,0:T(8,128)S(1)} %get-tuple-element.110), channel_id=1, source_target_pairs={{8,0},{16,8},{24,16},{9,1},{17,9},{25,17},{10,2},{18,10},{26,18},{... | collective-permute-start | bytes 15368 | tf_op jit(solution)/shard_map/ppermute | solution.py:33
  43.1 10.3 %collective-permute-start.10 = (f32[36,10]{1,0:T(8,128)S(1)}, f32[36,10]{1,0:T(8,128)S(1)}, u32[]{:S(2)}, u32[]{:S(2)}) collective-permute-start(f32[36,10]{1,0:T(8,128)S(1)} %get-tuple-element.101), channel_id=1, source_target_pairs={{0,1},{1,2},{2,3},{3,4},{4,5},{5,6},{6,7},{8,9},{9,10},{10,11},{11... | collective-permute-start | bytes 4328 | tf_op jit(solution)/shard_map/ppermute | solution.py:31
  46.6 8.8 %collective-permute-start.11 = (f32[36,10]{1,0:T(8,128)S(1)}, f32[36,10]{1,0:T(8,128)S(1)}, u32[]{:S(2)}, u32[]{:S(2)}) collective-permute-start(f32[36,10]{1,0:T(8,128)S(1)} %get-tuple-element.102), channel_id=1, source_target_pairs={{1,0},{2,1},{3,2},{4,3},{5,4},{6,5},{7,6},{9,8},{10,9},{11,10},{12... | collective-permute-start | bytes 4328 | tf_op jit(solution)/shard_map/ppermute | solution.py:33
  49.1 12.6 %collective-permute-start.6 = (f32[36,10]{1,0:T(8,128)S(1)}, f32[36,10]{1,0:T(8,128)S(1)}, u32[]{:S(2)}, u32[]{:S(2)}) collective-permute-start(f32[36,10]{1,0:T(8,128)S(1)} %get-tuple-element.103), channel_id=1, source_target_pairs={{0,1},{1,2},{2,3},{3,4},{4,5},{5,6},{6,7},{8,9},{9,10},{10,11},{11... | collective-permute-start | bytes 4328 | tf_op jit(solution)/shard_map/ppermute | solution.py:31
  53.4 8.3 %collective-permute-start.7 = (f32[36,10]{1,0:T(8,128)S(1)}, f32[36,10]{1,0:T(8,128)S(1)}, u32[]{:S(2)}, u32[]{:S(2)}) collective-permute-start(f32[36,10]{1,0:T(8,128)S(1)} %get-tuple-element.104), channel_id=1, source_target_pairs={{1,0},{2,1},{3,2},{4,3},{5,4},{6,5},{7,6},{9,8},{10,9},{11,10},{12... | collective-permute-start | bytes 4328 | tf_op jit(solution)/shard_map/ppermute | solution.py:33
  63.4 0.8 copy-start.4
  64.2 7.4 %copy-start.3 = (f32[132,1024]{0,1:T(8,128)}, f32[132,1024]{0,1:T(8,128)S(1)}, u32[]{:S(2)}) copy-start(f32[132,1024]{0,1:T(8,128)S(1)} %pad_maximum_fusion.1) | copy-start | bytes 1622020
  64.2 7.4 %collective-permute-start.2 = (f32[132,2]{0,1:T(2,128)S(1)}, f32[132,2]{0,1:T(2,128)S(1)}, u32[]{:S(2)}, u32[]{:S(2)}) collective-permute-start(f32[132,2]{0,1:T(2,128)S(1)} %get-tuple-element.33), channel_id=1, source_target_pairs={{0,1},{1,2},{2,3},{3,4},{4,5},{5,6},{6,7},{8,9},{9,10},{10,11},{11... | collective-permute-start | bytes 3176 | tf_op jit(solution)/shard_map/ppermute | solution.py:31
  69.0 6.4 %collective-permute-start.3 = (f32[132,2]{0,1:T(2,128)S(1)}, f32[132,2]{0,1:T(2,128)S(1)}, u32[]{:S(2)}, u32[]{:S(2)}) collective-permute-start(f32[132,2]{0,1:T(2,128)S(1)} %get-tuple-element.34), channel_id=1, source_target_pairs={{1,0},{2,1},{3,2},{4,3},{5,4},{6,5},{7,6},{9,8},{10,9},{11,10},{12... | collective-permute-start | bytes 3176 | tf_op jit(solution)/shard_map/ppermute | solution.py:33
  71.2 4.2 %copy-start.5 = (f32[2,1024]{0,1:T(8,128)S(1)}, f32[2,1024]{0,1:T(8,128)}, u32[]{:S(2)}) copy-start(f32[2,1024]{0,1:T(8,128)} %copy-done.4) | copy-start | bytes 24580
  92.3 3.3 %copy-start = (f32[8,130,1026]{1,2,0:T(8,128)}, f32[8,130,1026]{1,2,0:T(8,128)S(1)}, u32[]{:S(2)}) copy-start(f32[8,130,1026]{1,2,0:T(8,128)S(1)} %bitcast_dynamic-update-slice_fusion) | copy-start | bytes 12804484
  99.8 1.0 %copy-start.2 = (s32[128,1024]{0,1:T(8,128)S(1)}, s32[128,1024]{0,1:T(8,128)}, u32[]{:S(2)}) copy-start(s32[128,1024]{0,1:T(8,128)} %copy-done.1) | copy-start | bytes 1572868
where the time goes:
time: 104 us; the launch traced here: 103 us
  starting transfers between devices  35.6 us (34%)
  other arithmetic  35.2 us (34%)
  local copies, waits for them, and re-layouts  27.9 us (27%)
  waiting for transfers between devices  3.84 us (4%)
    ppermute x6, starting transfers between devices, with_halo(): lax.ppermute(tail, axis, [(i, (i + 1) % count) for i in range(ends)])  18.3 us
    ppermute x6, starting transfers between devices, with_halo(): lax.ppermute(head, axis, [((i + 1) % count, i) for i in range(ends)])  17.3 us
    add x2, other arithmetic, outflow_weight_matrix(): totals = jnp.sum(slopes, axis=0) + RETENTION  16 us
    reshape x1, local copies, waits for them, and re-layouts, on_device(): (valid_flag * elevation).reshape(coarse_rows, 8, coarse_cols, 8)  6.22 us
    reshape x1, local copies, waits for them, and re-layouts, on_device(): counts = valid_flag.reshape(coarse_rows, 8, coarse_cols, 8).sum(axis=(1, 3))  6.14 us
    unnamed x36, local copies, waits for them, and re-layouts  5.01 us
    div x2, other arithmetic, outflow_weight_matrix(): return slopes / totals  4.13 us
    reduce_sum x1, other arithmetic, on_device(): counts = valid_flag.reshape(coarse_rows, 8, coarse_cols, 8).sum(axis=(1, 3))  4.02 us
  transfers between devices with their start and end apart: 12, of which 1 were waited for; matrix products, arithmetic and copies ran while one was open for 32% of the time, Pallas kernels for 0%

commit v1 on v0

v1 whole, which is shorter than its diff:
```python
import functools

import jax
import jax.numpy as jnp
from jax import lax
from jax.experimental import pallas as pl
from jax.experimental.pallas import tpu as pltpu
from jax.sharding import PartitionSpec as P

ITERS = 8
OFFSETS = ((0, 1), (1, 1), (1, 0), (1, -1), (0, -1), (-1, -1), (-1, 0), (-1, 1))
RECIPROCAL = (1.0, 0.7071067811865476) * 4
RETENTION = 0.1
OUTSIDE = 1000.0
LANES = 128
F32 = jnp.float32


def coefficients(tie_ref):
    out = []
    for k in range(8):
        value = jnp.float32(0.0)
        for i in range(8):
            place = jnp.float32((1.0 + 0.5 * (7.0 - i) / 7.0) * RECIPROCAL[k])
            value = jnp.where(tie_ref[i] == k, place, value)
        out.append(value)
    return out


def shift_lanes(before, here, after, step, lane):
    if step == 0:
        return here
    if step < 0:
        return pltpu.roll(jnp.where(lane == LANES - 1, before, here), 1, 1)
    return pltpu.roll(jnp.where(lane == 0, after, here), LANES - 1, 1)


def take_lanes(values, index):
    return jnp.take_along_axis(values, index, axis=1, mode="promise_in_bounds")


def kernel(row_devices, col_devices, tie_ref, elev_ref, mask_ref, out_ref, zp, mask, recip, parts, ones,
           coarse, crecv, load_sem, send_sem, recv_sem):
    rows, cols = elev_ref.shape
    groups, blocks = rows // 8, cols // LANES
    row, col = lax.axis_index("rows"), lax.axis_index("cols")

    loads = []
    for j in range(blocks):
        part = pl.ds(j * LANES, LANES)
        loads.append(pltpu.make_async_copy(elev_ref.at[:, part], zp.at[j + 1, pl.ds(8, rows), :], load_sem.at[j]))
        loads.append(pltpu.make_async_copy(mask_ref.at[:, part], mask.at[j], load_sem.at[blocks + j]))
    for load in loads:
        load.start()

    barrier = pltpu.get_barrier_semaphore()
    exists = []
    for step_row, step_col in OFFSETS:
        there = jnp.bool_(True)
        if step_row > 0:
            there = row < row_devices - 1
        if step_row < 0:
            there = row > 0
        if step_col > 0:
            there = jnp.logical_and(there, col < col_devices - 1)
        if step_col < 0:
            there = jnp.logical_and(there, col > 0)
        exists.append(there)

    def peer(k):
        return {"rows": row + OFFSETS[k][0], "cols": col + OFFSETS[k][1]}

    for k in range(8):
        @pl.when(exists[k])
        def _():
            pl.semaphore_signal(barrier, inc=1, device_id=peer(k), device_id_type=pl.DeviceIdType.MESH)

    coef = coefficients(tie_ref)

    def halo(step_row, step_col):
        where_rows = {-1: pl.ds(0, 8), 0: pl.ds(8, rows), 1: pl.ds(8 + rows, 8)}[step_row]
        where_blocks = {-1: pl.ds(0, 1), 0: pl.ds(1, blocks), 1: pl.ds(blocks + 1, 1)}[step_col]
        return zp.at[where_blocks, where_rows, :]

    def edge(step_row, step_col):
        where_rows = {-1: pl.ds(8, 8), 0: pl.ds(8, rows), 1: pl.ds(rows, 8)}[step_row]
        where_blocks = {-1: pl.ds(1, 1), 0: pl.ds(1, blocks), 1: pl.ds(blocks, 1)}[step_col]
        return zp.at[where_blocks, where_rows, :]

    crows = groups
    for k in range(8):
        @pl.when(jnp.logical_not(exists[k]))
        def _():
            region = halo(*OFFSETS[k])
            region[...] = jnp.full(region.shape, OUTSIDE, F32)
            crecv[k, 0:crows, :] = jnp.full((crows, LANES), OUTSIDE, F32)
            crecv[k, crows:2 * crows, :] = jnp.zeros((crows, LANES), F32)

    ones[...] = (
        lax.broadcasted_iota(jnp.int32, (cols, LANES), 0) // 8 == lax.broadcasted_iota(jnp.int32, (cols, LANES), 1)
    ).astype(F32).astype(jnp.bfloat16)

    for load in loads:
        load.wait()

    total = jnp.zeros((4 * crows, LANES), F32)
    for j in range(blocks):
        height_sum = jnp.zeros((crows, LANES), F32)
        count_sum = jnp.zeros((crows, LANES), F32)
        for s in range(8):
            valid = mask[j, pl.ds(s, crows, stride=8), :].astype(F32)
            height_sum = height_sum + valid * zp[j + 1, pl.ds(8 + s, crows, stride=8), :]
            count_sum = count_sum + valid
        high = height_sum.astype(jnp.bfloat16)
        rest = height_sum - high.astype(F32)
        middle = rest.astype(jnp.bfloat16)
        low = (rest - middle.astype(F32)).astype(jnp.bfloat16)
        stacked = jnp.concatenate([count_sum.astype(jnp.bfloat16), high, middle, low], axis=0)
        total = total + jnp.dot(stacked, ones[j * LANES:(j + 1) * LANES, :], preferred_element_type=F32)
    counts = total[0:crows]
    heights = total[crows:2 * crows] + (total[2 * crows:3 * crows] + total[3 * crows:])
    overview = heights / (counts + 1.0)
    runoff = counts * (1.0 / 64.0)
    coarse[0:crows, :] = overview
    coarse[crows:2 * crows, :] = runoff

    pl.semaphore_wait(barrier, functools.reduce(jnp.add, [there.astype(jnp.int32) for there in exists]))

    def copies(k):
        opposite = (k + 4) % 8
        small = pltpu.make_async_remote_copy(
            src_ref=coarse, dst_ref=crecv.at[opposite], send_sem=send_sem.at[k], recv_sem=recv_sem.at[opposite],
            device_id=peer(k), device_id_type=pl.DeviceIdType.MESH)
        step_row, step_col = OFFSETS[k]
        large = pltpu.make_async_remote_copy(
            src_ref=edge(step_row, step_col), dst_ref=halo(-step_row, -step_col),
            send_sem=send_sem.at[8 + k], recv_sem=recv_sem.at[8 + opposite],
            device_id=peer(k), device_id_type=pl.DeviceIdType.MESH)
        return small, large

    def arrivals(k):
        small = pltpu.make_async_remote_copy(
            src_ref=coarse, dst_ref=crecv.at[k], send_sem=send_sem.at[k], recv_sem=recv_sem.at[k],
            device_id=peer(k), device_id_type=pl.DeviceIdType.MESH)
        step_row, step_col = OFFSETS[k]
        large = pltpu.make_async_remote_copy(
            src_ref=edge(step_row, step_col), dst_ref=halo(step_row, step_col),
            send_sem=send_sem.at[8 + k], recv_sem=recv_sem.at[8 + k],
            device_id=peer(k), device_id_type=pl.DeviceIdType.MESH)
        return small, large

    for which in range(2):
        for k in (1, 3, 5, 7, 0, 4, 2, 6):
            @pl.when(exists[k])
            def _():
                copies(k)[which].start()

    for k in range(8):
        @pl.when(exists[k])
        def _():
            arrivals(k)[1].wait_recv()

    lane = lax.broadcasted_iota(jnp.int32, (8, LANES), 1)
    sub = lax.broadcasted_iota(jnp.int32, (8, LANES), 0)

    def first_pass(g, carry):
        for j in range(blocks + 2):
            here = zp[j, pl.ds(8 * g + 7, 8), :]
            summed = jnp.full((8, LANES), RETENTION, F32)
            for step_row in (-1, 0, 1):
                at = pl.ds(8 * g + 7 + step_row, 8)
                line = [zp[min(max(b, 0), blocks + 1), at, :] for b in (j - 1, j, j + 1)]
                for k, (off_row, off_col) in enumerate(OFFSETS):
                    if off_row == step_row:
                        beside = shift_lanes(*line, off_col, lane)
                        summed = summed + coef[k] * jnp.maximum(here - beside, 0.0)
            recip[j, pl.ds(8 * g + 7, 8), :] = 1.0 / summed
        return carry

    lax.fori_loop(0, groups + 1, first_pass, 0)

    def second_pass(g, carry):
        for j in range(1, blocks + 1):
            here = zp[j, pl.ds(pl.multiple_of(8 * g + 8, 8), 8), :]
            inside, rim = {}, {}
            for step_col in (-1, 0, 1):
                terms = {}
                for step_row in (-1, 0, 1):
                    if (step_row, step_col) == (0, 0):
                        continue
                    k = OFFSETS.index((-step_row, -step_col))
                    at = pl.ds(8 * g + 8 + step_row, 8)
                    source = shift_lanes(zp[j - 1, at, :], zp[j, at, :], zp[j + 1, at, :], step_col, lane)
                    scale = shift_lanes(recip[j - 1, at, :], recip[j, at, :], recip[j + 1, at, :], step_col, lane)
                    terms[step_row] = coef[k] * jnp.maximum(source - here, 0.0) * scale
                inside[step_col] = jnp.where(sub == 0, 0.0, terms[-1]) + jnp.where(sub == 7, 0.0, terms[1])
                if step_col != 0:
                    inside[step_col] = inside[step_col] + terms[0]
                rim[step_col] = jnp.where(sub == 0, terms[-1], jnp.where(sub == 7, terms[1], 0.0))
            first, last = (lane & 7) == 0, (lane & 7) == 7
            at = pl.ds(pl.multiple_of(8 * g, 8), 8)
            for number, field in enumerate((inside, rim)):
                parts[2 * number, j - 1, at, :] = (
                    field[0] + jnp.where(first, 0.0, field[-1]) + jnp.where(last, 0.0, field[1])
                )
                parts[2 * number + 1, j - 1, at, :] = jnp.where(first, field[-1], jnp.where(last, field[1], 0.0))
        return carry

    lax.fori_loop(0, groups, second_pass, 0)

    for k in range(8):
        @pl.when(exists[k])
        def _():
            arrivals(k)[0].wait_recv()

    lane_c = lax.broadcasted_iota(jnp.int32, (crows, LANES), 1)
    half = crows // 2

    def window(base):
        def side(right, left):
            return jnp.where(
                lane_c < LANES // 2, crecv[right, base:base + crows, :], crecv[left, base:base + crows, :])

        own = jnp.concatenate([coarse[base:base + crows, :], side(0, 4)], axis=1)
        below = jnp.concatenate([crecv[2, base:base + crows, :], side(1, 3)], axis=1)
        above = jnp.concatenate([crecv[6, base:base + crows, :], side(7, 5)], axis=1)
        sub_w = lax.broadcasted_iota(jnp.int32, (8, 2 * LANES), 0)
        mixed = jnp.where(sub_w < 4, below[8:16], above[crows - 16:crows - 8])
        return jnp.concatenate([own, below[0:8], mixed, above[crows - 8:crows]], axis=0)

    z = window(0)
    supply = window(crows)
    high, wide = z.shape

    def turn(x, step, axis):
        return x if step == 0 else pltpu.roll(x, (-step) % x.shape[axis], axis)

    turned = {step: turn(z, step, 1) for step in (-1, 0, 1)}
    slopes = []
    for k, (step_row, step_col) in enumerate(OFFSETS):
        slopes.append(coef[k] * jnp.maximum(z - turn(turned[step_col], step_row, 0), 0.0))
    share = 1.0 / (functools.reduce(jnp.add, slopes) + RETENTION)
    weight = {}
    for k, (step_row, step_col) in enumerate(OFFSETS):
        weight[step_row, step_col] = turn(slopes[k] * share, -step_col, 1)
    flow = supply
    for _ in range(ITERS):
        moved = {step: turn(flow, -step, 1) for step in (-1, 0, 1)}
        sums = {}
        for step_row in (-1, 0, 1):
            sums[step_row] = functools.reduce(
                jnp.add, [weight[step_row, c] * moved[c] for c in (-1, 0, 1) if (step_row, c) in weight])
        flow = supply + sums[0] + turn(sums[1], -1, 0) + turn(sums[-1], 1, 0)

    left = turn(flow, -1, 1)[:, :LANES]
    right = turn(flow, 1, 1)[:, :LANES]
    centre = flow[:, :LANES]
    first, last = (lane & 7) == 0, (lane & 7) == 7
    per_block = LANES // 8
    for j in range(blocks):
        index = lane // 8 + j * per_block
        spread = []
        for at in list(range(0, crows, 8)) + [crows, high - 8]:
            mid = take_lanes(centre[at:at + 8], index)
            beside = jnp.where(first, take_lanes(left[at:at + 8], index), take_lanes(right[at:at + 8], index))
            spread.append((mid, beside))
        for g in range(groups):
            def level(number, group):
                where_at = {-1: (len(spread) - 1, 7), groups: (len(spread) - 2, 0)}.get(group, (group // 8, group % 8))
                line = spread[where_at[0]][number][where_at[1]:where_at[1] + 1, :]
                return jnp.broadcast_to(line, (8, LANES))

            at = slice(8 * g, 8 * g + 8)
            value = mask[j, at, :].astype(F32)
            for number in range(2):
                value = value + parts[number, j, at, :] * level(number, g)
                rim = jnp.where(sub == 0, level(number, g - 1), level(number, g + 1))
                value = value + parts[2 + number, j, at, :] * rim
            out_ref[at, j * LANES:(j + 1) * LANES] = value

    for k in range(8):
        @pl.when(exists[k])
        def _():
            small, large = copies(k)
            small.wait_send()
            large.wait_send()


def solution(mesh):
    row_devices, col_devices = mesh.shape["rows"], mesh.shape["cols"]

    def on_device(elevation, data_mask, tie_order):
        rows, cols = elevation.shape
        groups, blocks = rows // 8, cols // LANES
        return pl.pallas_call(
            functools.partial(kernel, row_devices, col_devices),
            out_shape=jax.ShapeDtypeStruct((rows, cols), F32),
            in_specs=[
                pl.BlockSpec(memory_space=pltpu.SMEM),
                pl.BlockSpec(memory_space=pl.ANY),
                pl.BlockSpec(memory_space=pl.ANY),
            ],
            out_specs=pl.BlockSpec(memory_space=pltpu.VMEM),
            scratch_shapes=[
                pltpu.VMEM((blocks + 2, rows + 16, LANES), F32),
                pltpu.VMEM((blocks, rows, LANES), jnp.int32),
                pltpu.VMEM((blocks + 2, rows + 16, LANES), F32),
                pltpu.VMEM((4, blocks, rows, LANES), F32),
                pltpu.VMEM((cols, LANES), jnp.bfloat16),
                pltpu.VMEM((2 * groups, LANES), F32),
                pltpu.VMEM((8, 2 * groups, LANES), F32),
                pltpu.SemaphoreType.DMA((2 * blocks,)),
                pltpu.SemaphoreType.DMA((16,)),
                pltpu.SemaphoreType.DMA((16,)),
            ],
            compiler_params=pltpu.CompilerParams(collective_id=0, has_side_effects=True),
        )(tie_order, elevation, data_mask)

    return jax.shard_map(
        on_device, mesh=mesh, in_specs=(P("rows", "cols"), P("rows", "cols"), P()),
        out_specs=P("rows", "cols"), check_vma=False)
```

time: 104 us -> 20.1 us (0.19)
  the two profiles are of different devices: /device:TPU:6 before, /device:TPU:9 now
where the time goes in v1:
time: 20.1 us; the launch traced here: 19.8 us
  Pallas kernels  17.9 us (89%)
  local copies, waits for them, and re-layouts  1.89 us (9%)
    pallas_call x1, Pallas kernels, on_device(): pl.pallas_call(functools.partial(kernel, row_devices, col_devices), out_s...  17.9 us
    unnamed x1, local copies, waits for them, and re-layouts  1.89 us

profile of v1, /device:TPU:9, one launch (start us, length us, event | category | flops | bytes accessed | tf_op | source)
XLA Modules:
  0.0 19.8 jit_solution(14722761638034531292)
XLA Ops:
  0.0 17.9 %shard_map.37 = f32[128,1024]{1,0:T(8,128)} custom-call(s32[8]{0:T(128)} %tie_ref.1, f32[128,1024]{1,0:T(8,128)} %elev_ref.1, s32[128,1024]{1,0:T(8,128)} %mask_ref.1), custom_call_target="tpu_custom_call" | custom-call | tf_op jit(solution)/shard_map/pallas_call | solution.py:295
  17.9 1.9 %copy.5 = f32[128,1024]{1,0:T(8,128)} copy(f32[128,1024]{1,0:T(8,128)} %shard_map.37) | data formatting | bytes 1048576

commit v2 on v1

v2 whole, which is shorter than its diff:
```python
import functools

import jax
import jax.numpy as jnp
from jax import lax
from jax.experimental import pallas as pl
from jax.experimental.pallas import tpu as pltpu
from jax.sharding import PartitionSpec as P

ITERS = 8
OFFSETS = ((0, 1), (1, 1), (1, 0), (1, -1), (0, -1), (-1, -1), (-1, 0), (-1, 1))
RECIPROCAL = (1.0, 0.7071067811865476) * 4
RETENTION = 0.1
OUTSIDE = 1000.0
LANES = 128
F32 = jnp.float32


def coefficients(tie_ref):
    out = []
    for k in range(8):
        value = jnp.float32(0.0)
        for i in range(8):
            place = jnp.float32((1.0 + 0.5 * (7.0 - i) / 7.0) * RECIPROCAL[k])
            value = jnp.where(tie_ref[i] == k, place, value)
        out.append(value)
    return out


def shift_lanes(before, here, after, step, lane):
    if step == 0:
        return here
    if step < 0:
        return pltpu.roll(jnp.where(lane == LANES - 1, before, here), 1, 1)
    return pltpu.roll(jnp.where(lane == 0, after, here), LANES - 1, 1)


def take_lanes(values, index):
    return jnp.take_along_axis(values, index, axis=1, mode="promise_in_bounds")


def kernel(row_devices, col_devices, tie_hbm, elev_ref, mask_ref, out_ref, tie_ref, zp, mask, recip, parts, ones,
           coarse, side, srecv, vrecv, load_sem, tie_sem, send_sem, recv_sem):
    rows, cols = elev_ref.shape
    groups, blocks = rows // 8, cols // LANES
    crows = groups
    row, col = lax.axis_index("rows"), lax.axis_index("cols")
    ring, rim = 0, blocks + 1

    loads = []
    for j in range(blocks):
        part = pl.ds(j * LANES, LANES)
        loads.append((
            pltpu.make_async_copy(elev_ref.at[:, part], zp.at[j + 1, pl.ds(8, rows), :], load_sem.at[j]),
            pltpu.make_async_copy(mask_ref.at[:, part], mask.at[j], load_sem.at[blocks + j])))
        loads[-1][0].start()
        loads[-1][1].start()
    tie_load = pltpu.make_async_copy(tie_hbm, tie_ref, tie_sem)
    tie_load.start()

    barrier = pltpu.get_barrier_semaphore()
    exists = []
    for step_row, step_col in OFFSETS:
        there = jnp.bool_(True)
        if step_row > 0:
            there = row < row_devices - 1
        if step_row < 0:
            there = row > 0
        if step_col > 0:
            there = jnp.logical_and(there, col < col_devices - 1)
        if step_col < 0:
            there = jnp.logical_and(there, col > 0)
        exists.append(there)

    def peer(k):
        return {"rows": row + OFFSETS[k][0], "cols": col + OFFSETS[k][1]}

    for k in range(8):
        @pl.when(exists[k])
        def _():
            pl.semaphore_signal(barrier, inc=1, device_id=peer(k), device_id_type=pl.DeviceIdType.MESH)

    lane = lax.broadcasted_iota(jnp.int32, (8, LANES), 1)
    sub = lax.broadcasted_iota(jnp.int32, (8, LANES), 0)
    lane_c = lax.broadcasted_iota(jnp.int32, (crows, LANES), 1)
    middle_lanes = jnp.logical_and(lane_c >= LANES // 4, lane_c < 3 * LANES // 4)

    SIDES, UPDOWN = (0, 1, 3, 4, 5, 7), (2, 6)

    def halo_rows(k):
        return zp.at[pl.ds(1, blocks), pl.ds(8 + rows if k == 2 else 0, 8), :]

    def edge_rows(k):
        return zp.at[pl.ds(1, blocks), pl.ds(rows if k == 2 else 8, 8), :]

    for k in range(8):
        @pl.when(jnp.logical_not(exists[k]))
        def _():
            if k in UPDOWN:
                region = halo_rows(k)
                region[...] = jnp.full(region.shape, OUTSIDE, F32)
                vrecv[k // 4, 0:crows, :] = jnp.full((crows, LANES), OUTSIDE, F32)
                vrecv[k // 4, crows:2 * crows, :] = jnp.zeros((crows, LANES), F32)
            else:
                srecv[k, 0:crows, :] = jnp.where(middle_lanes, 0.0, OUTSIDE)
                srecv[k, crows:crows + 8, :] = jnp.full((8, LANES), OUTSIDE, F32)

    ones[...] = (
        lax.broadcasted_iota(jnp.int32, (cols, LANES), 0) // 8 == lax.broadcasted_iota(jnp.int32, (cols, LANES), 1)
    ).astype(F32).astype(jnp.bfloat16)

    total = jnp.zeros((4 * crows, LANES), F32)
    for j in range(blocks):
        loads[j][0].wait()
        loads[j][1].wait()
        height_sum = jnp.zeros((crows, LANES), F32)
        count_sum = jnp.zeros((crows, LANES), F32)
        for s in range(8):
            valid = mask[j, pl.ds(s, crows, stride=8), :].astype(F32)
            height_sum = height_sum + valid * zp[j + 1, pl.ds(8 + s, crows, stride=8), :]
            count_sum = count_sum + valid
        high = height_sum.astype(jnp.bfloat16)
        rest = height_sum - high.astype(F32)
        middle = rest.astype(jnp.bfloat16)
        low = (rest - middle.astype(F32)).astype(jnp.bfloat16)
        stacked = jnp.concatenate([count_sum.astype(jnp.bfloat16), high, middle, low], axis=0)
        total = total + jnp.dot(stacked, ones[j * LANES:(j + 1) * LANES, :], preferred_element_type=F32)
    counts = total[0:crows]
    heights = total[crows:2 * crows] + (total[2 * crows:3 * crows] + total[3 * crows:])
    overview = heights / (counts + 1.0)
    runoff = counts * (1.0 / 64.0)

    packed = jnp.zeros((8, LANES), F32)
    for g in range(groups):
        at = pl.ds(8 + 8 * g, 8)
        edges = jnp.where(lane < LANES // 2, zp[1, at, :], zp[blocks, at, :])
        zp[rim, at, :] = edges
        packed = jnp.where(lane // 4 == g, pltpu.roll(edges, (2 + 4 * g) % LANES, 1), packed)
    side[crows:crows + 8, :] = packed
    side[0:crows, :] = jnp.where(middle_lanes, pltpu.roll(runoff, LANES // 2, 1), overview)
    coarse[0:crows, :] = overview
    coarse[crows:2 * crows, :] = runoff

    pl.semaphore_wait(barrier, functools.reduce(jnp.add, [there.astype(jnp.int32) for there in exists]))

    def copies(k, arriving=False):
        slot = k if arriving else (k + 4) % 8

        def remote(src, dst, extra):
            return pltpu.make_async_remote_copy(
                src_ref=src, dst_ref=dst, send_sem=send_sem.at[k + extra], recv_sem=recv_sem.at[slot + extra],
                device_id=peer(k), device_id_type=pl.DeviceIdType.MESH)

        if k in UPDOWN:
            return [remote(coarse, vrecv.at[slot // 4], 0), remote(edge_rows(k), halo_rows(slot), 8)]
        return [remote(side, srecv.at[slot], 0)]

    for k in (1, 3, 5, 7, 0, 4, 2, 6):
        @pl.when(exists[k])
        def _():
            for copy in copies(k):
                copy.start()

    tie_load.wait()
    coef = coefficients(tie_ref)

    def first_pass(g, around):
        for j, before, after in around:
            here = zp[j, pl.ds(8 * g + 7, 8), :]
            summed = jnp.full((8, LANES), RETENTION, F32)
            for step_row in (-1, 0, 1):
                at = pl.ds(8 * g + 7 + step_row, 8)
                line = [zp[b, at, :] for b in (before, j, after)]
                for k, (off_row, off_col) in enumerate(OFFSETS):
                    if off_row == step_row:
                        beside = shift_lanes(*line, off_col, lane)
                        summed = summed + coef[k] * jnp.maximum(here - beside, 0.0)
            recip[j, pl.ds(8 * g + 7, 8), :] = 1.0 / summed

    def second_pass(g, around, store):
        for j, before, after in around:
            here = zp[j, pl.ds(8 * g + 8, 8), :]
            inside, outer = {}, {}
            for step_col in (-1, 0, 1):
                terms = {}
                for step_row in (-1, 0, 1):
                    if (step_row, step_col) == (0, 0):
                        continue
                    k = OFFSETS.index((-step_row, -step_col))
                    at = pl.ds(8 * g + 8 + step_row, 8)
                    source = shift_lanes(zp[before, at, :], zp[j, at, :], zp[after, at, :], step_col, lane)
                    scale = shift_lanes(recip[before, at, :], recip[j, at, :], recip[after, at, :], step_col, lane)
                    terms[step_row] = coef[k] * jnp.maximum(source - here, 0.0) * scale
                inside[step_col] = jnp.where(sub == 0, 0.0, terms[-1]) + jnp.where(sub == 7, 0.0, terms[1])
                if step_col != 0:
                    inside[step_col] = inside[step_col] + terms[0]
                outer[step_col] = jnp.where(sub == 0, terms[-1], jnp.where(sub == 7, terms[1], 0.0))
            first, last = (lane & 7) == 0, (lane & 7) == 7
            for number, field in enumerate((inside, outer)):
                store(g, j, 2 * number, field[0] + jnp.where(first, 0.0, field[-1]) + jnp.where(last, 0.0, field[1]))
                store(g, j, 2 * number + 1, jnp.where(first, field[-1], jnp.where(last, field[1], 0.0)))

    def keep(g, j, number, value):
        parts[number, j - 1, pl.ds(8 * g, 8), :] = value

    def keep_edges(g, j, number, value):
        at = pl.ds(8 * g, 8)
        parts[number, 0, at, :] = jnp.where(lane < 8, value, parts[number, 0, at, :])
        parts[number, blocks - 1, at, :] = jnp.where(lane >= LANES - 8, value, parts[number, blocks - 1, at, :])

    own = [(j, j - 1, j + 1 if j < blocks else ring) for j in range(1, blocks + 1)]
    outside, edges = (ring, blocks, 1), (rim, ring, ring)

    def loop(start, stop, body):
        def step(g, carry):
            body(g)
            return carry

        lax.fori_loop(start, stop, step, 0)

    loop(1, groups, lambda g: first_pass(g, own))
    loop(1, groups - 1, lambda g: second_pass(g, own, keep))

    for k in range(8):
        @pl.when(exists[k])
        def _():
            for copy in copies(k, arriving=True):
                copy.wait_recv()

    def outside_columns(g, right, left):
        chosen = jnp.where(lane >= 4 * g + 2, srecv[right, crows:crows + 8, :], srecv[left, crows:crows + 8, :])
        return pltpu.roll(chosen, (2 * LANES - 4 * g - 2) % LANES, 1)

    for g in range(groups):
        zp[ring, pl.ds(8 + 8 * g, 8), :] = outside_columns(g, 0, 4)
    zp[ring, 0:8, :] = outside_columns(groups - 1, 7, 5)
    zp[ring, rows + 8:rows + 16, :] = outside_columns(0, 1, 3)
    for at in (0, rows + 8):
        zp[rim, at:at + 8, :] = jnp.where(lane < LANES // 2, zp[1, at:at + 8, :], zp[blocks, at:at + 8, :])
    loop(0, groups + 1, lambda g: first_pass(g, [outside, edges]))
    loop(0, 2, lambda i: first_pass(i * groups, own))
    loop(0, 2, lambda i: second_pass(i * (groups - 1), own, keep))
    loop(0, groups, lambda g: second_pass(g, [edges], keep_edges))

    half = LANES // 2

    def window(field):
        def beside(right, left):
            a, b = srecv[right, 0:crows, :], srecv[left, 0:crows, :]
            return jnp.where(lane_c < half, a, b) if field == 0 else pltpu.roll(jnp.where(lane_c < half, b, a), half, 1)

        at = slice(field * crows, (field + 1) * crows)
        here = jnp.concatenate([coarse[at, :], beside(0, 4)], axis=1)
        below = jnp.concatenate([vrecv[0, at, :], beside(1, 3)], axis=1)
        above = jnp.concatenate([vrecv[1, at, :], beside(7, 5)], axis=1)
        sub_w = lax.broadcasted_iota(jnp.int32, (8, 2 * LANES), 0)
        mixed = jnp.where(sub_w < 4, below[8:16], above[crows - 16:crows - 8])
        return jnp.concatenate([here, below[0:8], mixed, above[crows - 8:crows]], axis=0)

    z = window(0)
    supply = window(1)
    high = z.shape[0]

    def turn(x, step, axis):
        return x if step == 0 else pltpu.roll(x, (-step) % x.shape[axis], axis)

    turned = {step: turn(z, step, 1) for step in (-1, 0, 1)}
    slopes = []
    for k, (step_row, step_col) in enumerate(OFFSETS):
        slopes.append(coef[k] * jnp.maximum(z - turn(turned[step_col], step_row, 0), 0.0))
    share = 1.0 / (functools.reduce(jnp.add, slopes) + RETENTION)
    weight = {}
    for k, (step_row, step_col) in enumerate(OFFSETS):
        weight[step_row, step_col] = turn(slopes[k] * share, -step_col, 1)
    flow = supply
    for _ in range(ITERS):
        moved = {step: turn(flow, -step, 1) for step in (-1, 0, 1)}
        sums = {}
        for step_row in (-1, 0, 1):
            sums[step_row] = functools.reduce(
                jnp.add, [weight[step_row, c] * moved[c] for c in (-1, 0, 1) if (step_row, c) in weight])
        flow = supply + sums[0] + turn(sums[1], -1, 0) + turn(sums[-1], 1, 0)

    left = turn(flow, -1, 1)[:, :LANES]
    right = turn(flow, 1, 1)[:, :LANES]
    centre = flow[:, :LANES]
    first, last = (lane & 7) == 0, (lane & 7) == 7
    per_block = LANES // 8
    for j in range(blocks):
        index = lane // 8 + j * per_block
        spread = []
        for at in list(range(0, crows, 8)) + [crows, high - 8]:
            mid = take_lanes(centre[at:at + 8], index)
            beside = jnp.where(first, take_lanes(left[at:at + 8], index), take_lanes(right[at:at + 8], index))
            spread.append((mid, beside))
        for g in range(groups):
            def level(number, group):
                where_at = {-1: (len(spread) - 1, 7), groups: (len(spread) - 2, 0)}.get(group, (group // 8, group % 8))
                line = spread[where_at[0]][number][where_at[1]:where_at[1] + 1, :]
                return jnp.broadcast_to(line, (8, LANES))

            at = slice(8 * g, 8 * g + 8)
            value = mask[j, at, :].astype(F32)
            for number in range(2):
                value = value + parts[number, j, at, :] * level(number, g)
                across = jnp.where(sub == 0, level(number, g - 1), level(number, g + 1))
                value = value + parts[2 + number, j, at, :] * across
            out_ref[at, j * LANES:(j + 1) * LANES] = value

    for k in range(8):
        @pl.when(exists[k])
        def _():
            for copy in copies(k):
                copy.wait_send()


def solution(mesh):
    row_devices, col_devices = mesh.shape["rows"], mesh.shape["cols"]

    def on_device(elevation, data_mask, tie_order):
        rows, cols = elevation.shape
        groups, blocks = rows // 8, cols // LANES
        return pl.pallas_call(
            functools.partial(kernel, row_devices, col_devices),
            out_shape=jax.ShapeDtypeStruct((rows, cols), F32),
            in_specs=[pl.BlockSpec(memory_space=pl.ANY)] * 3,
            out_specs=pl.BlockSpec(memory_space=pltpu.VMEM),
            scratch_shapes=[
                pltpu.SMEM((8,), jnp.int32),
                pltpu.VMEM((blocks + 2, rows + 16, LANES), F32),
                pltpu.VMEM((blocks, rows, LANES), jnp.int32),
                pltpu.VMEM((blocks + 2, rows + 16, LANES), F32),
                pltpu.VMEM((4, blocks, rows, LANES), F32),
                pltpu.VMEM((cols, LANES), jnp.bfloat16),
                pltpu.VMEM((2 * groups, LANES), F32),
                pltpu.VMEM((groups + 8, LANES), F32),
                pltpu.VMEM((8, groups + 8, LANES), F32),
                pltpu.VMEM((2, 2 * groups, LANES), F32),
                pltpu.SemaphoreType.DMA((2 * blocks,)),
                pltpu.SemaphoreType.DMA,
                pltpu.SemaphoreType.DMA((16,)),
                pltpu.SemaphoreType.DMA((16,)),
            ],
            compiler_params=pltpu.CompilerParams(collective_id=0, has_side_effects=True),
        )(tie_order, elevation, data_mask)

    return jax.shard_map(
        on_device, mesh=mesh, in_specs=(P("rows", "cols"), P("rows", "cols"), P()),
        out_specs=P("rows", "cols"), check_vma=False)
```

time: 20.1 us -> 16.2 us (0.81)
  the two profiles are of different devices: /device:TPU:9 before, /device:TPU:1 now
where the time goes in v2:
time: 16.2 us; the launch traced here: 16 us
  Pallas kernels  14.1 us (87%)
  local copies, waits for them, and re-layouts  1.89 us (12%)
    pallas_call x1, Pallas kernels, on_device(): pl.pallas_call(functools.partial(kernel, row_devices, col_devices), out_s...  14.1 us
    unnamed x1, local copies, waits for them, and re-layouts  1.89 us

profile of v2, /device:TPU:1, one launch (start us, length us, event | category | flops | bytes accessed | tf_op | source)
XLA Modules:
  0.0 16.0 jit_solution(10722172869165939968)
XLA Ops:
  0.0 14.1 %shard_map.37 = f32[128,1024]{1,0:T(8,128)} custom-call(s32[8]{0:T(128)} %tie_hbm.1, f32[128,1024]{1,0:T(8,128)} %elev_ref.1, s32[128,1024]{1,0:T(8,128)} %mask_ref.1), custom_call_target="tpu_custom_call" | custom-call | tf_op jit(solution)/shard_map/pallas_call | solution.py:323
  14.1 1.9 %copy.5 = f32[128,1024]{1,0:T(8,128)} copy(f32[128,1024]{1,0:T(8,128)} %shard_map.37) | data formatting | bytes 1048576

commit v3 on v2

--- a/solution.py
+++ b/solution.py
@@ -39,7 +39,7 @@
     return jnp.take_along_axis(values, index, axis=1, mode="promise_in_bounds")
 
 
-def kernel(row_devices, col_devices, tie_hbm, elev_ref, mask_ref, out_ref, tie_ref, zp, mask, recip, parts, ones,
+def kernel(row_devices, col_devices, tie_hbm, elev_ref, mask_ref, out_ref, tie_ref, zp, zl, zr, mask, recip, rl, rr, parts, ones,
            coarse, side, srecv, vrecv, load_sem, tie_sem, send_sem, recv_sem):
     rows, cols = elev_ref.shape
     groups, blocks = rows // 8, cols // LANES
@@ -164,18 +164,30 @@
     tie_load.wait()
     coef = coefficients(tie_ref)
 
+    def beside_heights(at, around):
+        for j, before, after in around:
+            line = [zp[b, at, :] for b in (before, j, after)]
+            zl[j, at, :] = shift_lanes(*line, -1, lane)
+            zr[j, at, :] = shift_lanes(*line, 1, lane)
+
+    by_column = {-1: zl, 0: zp, 1: zr}
+    scale_by_column = {-1: rl, 0: recip, 1: rr}
+
     def first_pass(g, around):
+        done = {}
+        middle_at = pl.ds(8 * g + 7, 8)
         for j, before, after in around:
-            here = zp[j, pl.ds(8 * g + 7, 8), :]
+            here = zp[j, middle_at, :]
             summed = jnp.full((8, LANES), RETENTION, F32)
-            for step_row in (-1, 0, 1):
-                at = pl.ds(8 * g + 7 + step_row, 8)
-                line = [zp[b, at, :] for b in (before, j, after)]
-                for k, (off_row, off_col) in enumerate(OFFSETS):
-                    if off_row == step_row:
-                        beside = shift_lanes(*line, off_col, lane)
-                        summed = summed + coef[k] * jnp.maximum(here - beside, 0.0)
-            recip[j, pl.ds(8 * g + 7, 8), :] = 1.0 / summed
+            for k, (off_row, off_col) in enumerate(OFFSETS):
+                beside = by_column[off_col][j, pl.ds(8 * g + 7 + off_row, 8), :]
+                summed = summed + coef[k] * jnp.maximum(here - beside, 0.0)
+            done[j] = 1.0 / summed
+            recip[j, middle_at, :] = done[j]
+        for j, before, after in around:
+            line = [done.get(b, done[j]) for b in (before, j, after)]
+            rl[j, middle_at, :] = shift_lanes(*line, -1, lane)
+            rr[j, middle_at, :] = shift_lanes(*line, 1, lane)
 
     def second_pass(g, around, store):
         for j, before, after in around:
@@ -188,8 +200,8 @@
                         continue
                     k = OFFSETS.index((-step_row, -step_col))
                     at = pl.ds(8 * g + 8 + step_row, 8)
-                    source = shift_lanes(zp[before, at, :], zp[j, at, :], zp[after, at, :], step_col, lane)
-                    scale = shift_lanes(recip[before, at, :], recip[j, at, :], recip[after, at, :], step_col, lane)
+                    source = by_column[step_col][j, at, :]
+                    scale = scale_by_column[step_col][j, at, :]
                     terms[step_row] = coef[k] * jnp.maximum(source - here, 0.0) * scale
                 inside[step_col] = jnp.where(sub == 0, 0.0, terms[-1]) + jnp.where(sub == 7, 0.0, terms[1])
                 if step_col != 0:
@@ -218,6 +230,7 @@
 
         lax.fori_loop(start, stop, step, 0)
 
+    loop(0, groups, lambda g: beside_heights(pl.ds(pl.multiple_of(8 * g + 8, 8), 8), own))
     loop(1, groups, lambda g: first_pass(g, own))
     loop(1, groups - 1, lambda g: second_pass(g, own, keep))
 
@@ -237,6 +250,9 @@
     zp[ring, rows + 8:rows + 16, :] = outside_columns(0, 1, 3)
     for at in (0, rows + 8):
         zp[rim, at:at + 8, :] = jnp.where(lane < LANES // 2, zp[1, at:at + 8, :], zp[blocks, at:at + 8, :])
+    for at in (0, rows + 8):
+        beside_heights(pl.ds(at, 8), own)
+    loop(0, groups + 2, lambda g: beside_heights(pl.ds(pl.multiple_of(8 * g, 8), 8), [outside, edges]))
     loop(0, groups + 1, lambda g: first_pass(g, [outside, edges]))
     loop(0, 2, lambda i: first_pass(i * groups, own))
     loop(0, 2, lambda i: second_pass(i * (groups - 1), own, keep))
@@ -328,7 +344,11 @@
             scratch_shapes=[
                 pltpu.SMEM((8,), jnp.int32),
                 pltpu.VMEM((blocks + 2, rows + 16, LANES), F32),
+                pltpu.VMEM((blocks + 2, rows + 16, LANES), F32),
+                pltpu.VMEM((blocks + 2, rows + 16, LANES), F32),
                 pltpu.VMEM((blocks, rows, LANES), jnp.int32),
+                pltpu.VMEM((blocks + 2, rows + 16, LANES), F32),
+                pltpu.VMEM((blocks + 2, rows + 16, LANES), F32),
                 pltpu.VMEM((blocks + 2, rows + 16, LANES), F32),
                 pltpu.VMEM((4, blocks, rows, LANES), F32),
                 pltpu.VMEM((cols, LANES), jnp.bfloat16),

time: 16.2 us -> 16 us (0.988)
  Pallas kernels: 14.1 us -> 13.9 us
    pallas_call x1, Pallas kernels: 14.1 us -> 13.9 us  [on_device(): pl.pallas_call(functools.partial(kernel, row_devices, col_devices), out_s...]
where the time goes in v3:
time: 16 us; the launch traced here: 15.8 us
  Pallas kernels  13.9 us (87%)
  local copies, waits for them, and re-layouts  1.89 us (12%)
    pallas_call x1, Pallas kernels, on_device(): pl.pallas_call(functools.partial(kernel, row_devices, col_devices), out_s...  13.9 us
    unnamed x1, local copies, waits for them, and re-layouts  1.89 us

profile of v3, /device:TPU:1, one launch (start us, length us, event | category | flops | bytes accessed | tf_op | source)
XLA Modules:
  0.0 15.8 jit_solution(4908923757916347239)
XLA Ops:
  0.0 13.9 %shard_map.37 = f32[128,1024]{1,0:T(8,128)} custom-call(s32[8]{0:T(128)} %tie_hbm.1, f32[128,1024]{1,0:T(8,128)} %elev_ref.1, s32[128,1024]{1,0:T(8,128)} %mask_ref.1), custom_call_target="tpu_custom_call" | custom-call | tf_op jit(solution)/shard_map/pallas_call | solution.py:339
  13.9 1.9 %copy.5 = f32[128,1024]{1,0:T(8,128)} copy(f32[128,1024]{1,0:T(8,128)} %shard_map.37) | data formatting | bytes 1048576

commit v4 on v3

--- a/solution.py
+++ b/solution.py
@@ -152,14 +152,16 @@
                 device_id=peer(k), device_id_type=pl.DeviceIdType.MESH)
 
         if k in UPDOWN:
-            return [remote(coarse, vrecv.at[slot // 4], 0), remote(edge_rows(k), halo_rows(slot), 8)]
-        return [remote(side, srecv.at[slot], 0)]
-
-    for k in (1, 3, 5, 7, 0, 4, 2, 6):
-        @pl.when(exists[k])
-        def _():
-            for copy in copies(k):
-                copy.start()
+            return remote(edge_rows(k), halo_rows(slot), 8), remote(coarse, vrecv.at[slot // 4], 0)
+        fine, wide = pl.ds(crows, 8), pl.ds(0, crows)
+        return (remote(side.at[fine, :], srecv.at[slot, fine, :], 8),
+                remote(side.at[wide, :], srecv.at[slot, wide, :], 0))
+
+    for which in range(2):
+        for k in (1, 3, 5, 7, 0, 4, 2, 6):
+            @pl.when(exists[k])
+            def _():
+                copies(k)[which].start()
 
     tie_load.wait()
     coef = coefficients(tie_ref)
@@ -234,11 +236,13 @@
     loop(1, groups, lambda g: first_pass(g, own))
     loop(1, groups - 1, lambda g: second_pass(g, own, keep))
 
-    for k in range(8):
-        @pl.when(exists[k])
-        def _():
-            for copy in copies(k, arriving=True):
-                copy.wait_recv()
+    def receive(which):
+        for k in range(8):
+            @pl.when(exists[k])
+            def _():
+                copies(k, arriving=True)[which].wait_recv()
+
+    receive(0)
 
     def outside_columns(g, right, left):
         chosen = jnp.where(lane >= 4 * g + 2, srecv[right, crows:crows + 8, :], srecv[left, crows:crows + 8, :])
@@ -257,6 +261,8 @@
     loop(0, 2, lambda i: first_pass(i * groups, own))
     loop(0, 2, lambda i: second_pass(i * (groups - 1), own, keep))
     loop(0, groups, lambda g: second_pass(g, [edges], keep_edges))
+
+    receive(1)
 
     half = LANES // 2
 
@@ -338,7 +344,7 @@
         groups, blocks = rows // 8, cols // LANES
         return pl.pallas_call(
             functools.partial(kernel, row_devices, col_devices),
-            out_shape=jax.ShapeDtypeStruct((rows, cols), F32),
+            out_shape=pltpu.VMEM((rows, cols), F32),
             in_specs=[pl.BlockSpec(memory_space=pl.ANY)] * 3,
             out_specs=pl.BlockSpec(memory_space=pltpu.VMEM),
             scratch_shapes=[
@@ -361,7 +367,7 @@
                 pltpu.SemaphoreType.DMA((16,)),
                 pltpu.SemaphoreType.DMA((16,)),
             ],
-            compiler_params=pltpu.CompilerParams(collective_id=0, has_side_effects=True),
+            compiler_params=pltpu.CompilerParams(collective_id=0, has_side_effects=True, vmem_limit_bytes=61000000),
         )(tie_order, elevation, data_mask)
 
     return jax.shard_map(

time: 16 us -> 14.1 us (0.88)
  local copies, waits for them, and re-layouts: 1.89 us -> 0.8 us
  Pallas kernels: 13.9 us -> 13.2 us
    unnamed x1, local copies, waits for them, and re-layouts: 1.89 us -> 0.8 us
    pallas_call x1, Pallas kernels: 13.9 us -> 13.2 us  [on_device(): pl.pallas_call(functools.partial(kernel, row_devices, col_devices), out_s...]
where the time goes in v4:
time: 14.1 us; the launch traced here: 14 us
  Pallas kernels  13.2 us (94%)
  local copies, waits for them, and re-layouts  0.8 us (6%)
    pallas_call x1, Pallas kernels, on_device(): pl.pallas_call(functools.partial(kernel, row_devices, col_devices), out_s...  13.2 us
    unnamed x1, local copies, waits for them, and re-layouts  0.8 us

profile of v4, /device:TPU:1, one launch (start us, length us, event | category | flops | bytes accessed | tf_op | source)
XLA Modules:
  0.0 14.0 jit_solution(6516077938258451737)
XLA Ops:
  0.0 13.2 %shard_map.37 = f32[128,1024]{1,0:T(8,128)S(1)} custom-call(s32[8]{0:T(128)} %tie_hbm.1, f32[128,1024]{1,0:T(8,128)} %elev_ref.1, s32[128,1024]{1,0:T(8,128)} %mask_ref.1), custom_call_target="tpu_custom_call" | custom-call | tf_op jit(solution)/shard_map/pallas_call | solution.py:345
  13.2 0.8 %copy.5 = f32[128,1024]{1,0:T(8,128)} copy(f32[128,1024]{1,0:T(8,128)S(1)} %shard_map.37) | data formatting | bytes 1048576

commit v5 on v4

--- a/solution.py
+++ b/solution.py
@@ -109,9 +109,43 @@
         lax.broadcasted_iota(jnp.int32, (cols, LANES), 0) // 8 == lax.broadcasted_iota(jnp.int32, (cols, LANES), 1)
     ).astype(F32).astype(jnp.bfloat16)
 
+    for load in loads:
+        load[0].wait()
+
+    packed = jnp.zeros((8, LANES), F32)
+    for g in range(groups):
+        at = pl.ds(8 + 8 * g, 8)
+        edges = jnp.where(lane < LANES // 2, zp[1, at, :], zp[blocks, at, :])
+        zp[rim, at, :] = edges
+        packed = jnp.where(lane // 4 == g, pltpu.roll(edges, (2 + 4 * g) % LANES, 1), packed)
+    side[crows:crows + 8, :] = packed
+
+    pl.semaphore_wait(barrier, functools.reduce(jnp.add, [there.astype(jnp.int32) for there in exists]))
+
+    def copies(k, arriving=False):
+        slot = k if arriving else (k + 4) % 8
+
+        def remote(src, dst, extra):
+            return pltpu.make_async_remote_copy(
+                src_ref=src, dst_ref=dst, send_sem=send_sem.at[k + extra], recv_sem=recv_sem.at[slot + extra],
+                device_id=peer(k), device_id_type=pl.DeviceIdType.MESH)
+
+        if k in UPDOWN:
+            return remote(edge_rows(k), halo_rows(slot), 8), remote(coarse, vrecv.at[slot // 4], 0)
+        fine, wide = pl.ds(crows, 8), pl.ds(0, crows)
+        return (remote(side.at[fine, :], srecv.at[slot, fine, :], 8),
+                remote(side.at[wide, :], srecv.at[slot, wide, :], 0))
+
+    def send(which):
+        for k in (1, 3, 5, 7, 0, 4, 2, 6):
+            @pl.when(exists[k])
+            def _():
+                copies(k)[which].start()
+
+    send(0)
+
     total = jnp.zeros((4 * crows, LANES), F32)
     for j in range(blocks):
-        loads[j][0].wait()
         loads[j][1].wait()
         height_sum = jnp.zeros((crows, LANES), F32)
         count_sum = jnp.zeros((crows, LANES), F32)
@@ -130,38 +164,11 @@
     overview = heights / (counts + 1.0)
     runoff = counts * (1.0 / 64.0)
 
-    packed = jnp.zeros((8, LANES), F32)
-    for g in range(groups):
-        at = pl.ds(8 + 8 * g, 8)
-        edges = jnp.where(lane < LANES // 2, zp[1, at, :], zp[blocks, at, :])
-        zp[rim, at, :] = edges
-        packed = jnp.where(lane // 4 == g, pltpu.roll(edges, (2 + 4 * g) % LANES, 1), packed)
-    side[crows:crows + 8, :] = packed
     side[0:crows, :] = jnp.where(middle_lanes, pltpu.roll(runoff, LANES // 2, 1), overview)
     coarse[0:crows, :] = overview
     coarse[crows:2 * crows, :] = runoff
 
-    pl.semaphore_wait(barrier, functools.reduce(jnp.add, [there.astype(jnp.int32) for there in exists]))
-
-    def copies(k, arriving=False):
-        slot = k if arriving else (k + 4) % 8
-
-        def remote(src, dst, extra):
-            return pltpu.make_async_remote_copy(
-                src_ref=src, dst_ref=dst, send_sem=send_sem.at[k + extra], recv_sem=recv_sem.at[slot + extra],
-                device_id=peer(k), device_id_type=pl.DeviceIdType.MESH)
-
-        if k in UPDOWN:
-            return remote(edge_rows(k), halo_rows(slot), 8), remote(coarse, vrecv.at[slot // 4], 0)
-        fine, wide = pl.ds(crows, 8), pl.ds(0, crows)
-        return (remote(side.at[fine, :], srecv.at[slot, fine, :], 8),
-                remote(side.at[wide, :], srecv.at[slot, wide, :], 0))
-
-    for which in range(2):
-        for k in (1, 3, 5, 7, 0, 4, 2, 6):
-            @pl.when(exists[k])
-            def _():
-                copies(k)[which].start()
+    send(1)
 
     tie_load.wait()
     coef = coefficients(tie_ref)

time: 14.1 us -> 14.7 us (1.043)
  Pallas kernels: 13.2 us -> 13.7 us
    pallas_call x1, Pallas kernels: 13.2 us -> 13.7 us  [on_device(): pl.pallas_call(functools.partial(kernel, row_devices, col_devices), out_s...]
where the time goes in v5:
time: 14.7 us; the launch traced here: 14.5 us
  Pallas kernels  13.7 us (93%)
  local copies, waits for them, and re-layouts  0.8 us (5%)
    pallas_call x1, Pallas kernels, on_device(): pl.pallas_call(functools.partial(kernel, row_devices, col_devices), out_s...  13.7 us
    unnamed x1, local copies, waits for them, and re-layouts  0.8 us

profile of v5, /device:TPU:1, one launch (start us, length us, event | category | flops | bytes accessed | tf_op | source)
XLA Modules:
  0.0 14.5 jit_solution(15437902267878756555)
XLA Ops:
  0.0 13.7 %shard_map.37 = f32[128,1024]{1,0:T(8,128)S(1)} custom-call(s32[8]{0:T(128)} %tie_hbm.1, f32[128,1024]{1,0:T(8,128)} %elev_ref.1, s32[128,1024]{1,0:T(8,128)} %mask_ref.1), custom_call_target="tpu_custom_call" | custom-call | tf_op jit(solution)/shard_map/pallas_call | solution.py:352
  13.7 0.8 %copy.5 = f32[128,1024]{1,0:T(8,128)} copy(f32[128,1024]{1,0:T(8,128)S(1)} %shard_map.37) | data formatting | bytes 1048576
